TPU v7x, 64 devices: a 2x2x8 block of a 4x4x8 slice. The times are simulated.
64 devices in a mesh: data: 4 (over x, y), ctx: 16 (over z, core).
Axes of the slice: x: 2, y: 2, z: 8, core: 2. Of those that a mesh axis runs over, the one named last changes fastest.
The devices are a block of a 4x4x8 slice.
Arguments:
- hidden: bfloat16 [2048, 5120], P(('data', 'ctx')), parts along dimension 0
- seq_lens: int32 [2048], P(('data', 'ctx')), parts along dimension 0
- w_query: bfloat16 [1, 5120, 5120], replicated
- w_key: bfloat16 [1, 5120, 1024], replicated
- w_value: bfloat16 [1, 5120, 1024], replicated
- w_out: bfloat16 [1, 5120, 5120], replicated
- k_prefix: bfloat16 [1, 16384, 8, 128], P(None, ('data', 'ctx')), parts along dimension 1
- v_prefix: bfloat16 [1, 16384, 8, 128], P(None, ('data', 'ctx')), parts along dimension 1
- k_suffix: bfloat16 [1, 2048, 32, 8, 128], P(None, ('data', 'ctx')), parts along dimension 1
- v_suffix: bfloat16 [1, 2048, 32, 8, 128], P(None, ('data', 'ctx')), parts along dimension 1
Outputs:
- output 1: bfloat16 [2048, 5120], P(('data', 'ctx')), parts along dimension 0
- output 2: bfloat16 [1, 2048, 32, 8, 128], P(None, ('data', 'ctx')), parts along dimension 1
- output 3: bfloat16 [1, 2048, 32, 8, 128], P(None, ('data', 'ctx')), parts along dimension 1
There are 4 independent parts. A program takes and returns all parts, laid end to end along the dimension named above; an argument that names none is the same for every part.
All inputs are finite; a program needn't handle non-finite values.
Results may differ from a plain program's by a relative error of at most 0.007338.
Values are sent between devices in bfloat16 or wider.
A program may use at most 768 MiB of HBM per device.

v0:
```python
import jax
import jax.numpy as jnp
from jax import lax
from jax.sharding import PartitionSpec as P


def solution(mesh):
    ctx_size = mesh.shape['ctx']
    home_axes = ('data', 'ctx')
    row_spec = P(home_axes, None)
    lens_spec = P(home_axes)
    whole_spec = P()
    prefix_spec = P(None, home_axes, None, None)
    cache_spec = P(None, home_axes, None, None, None)

    def local_step(hidden, seq_lens, w_query, w_key, w_value, w_out, k_prefix, v_prefix, k_suffix, v_suffix):
        layers = w_query.shape[0]
        kv_heads = k_prefix.shape[2]
        head_dim = k_prefix.shape[3]
        num_heads = w_query.shape[2] // head_dim
        group_size = num_heads // kv_heads
        home_rows = hidden.shape[0]
        slot_count = k_suffix.shape[2]
        score_scale = head_dim ** -0.5
        slot_ids = lax.broadcasted_iota(jnp.int32, (home_rows, slot_count), 1)
        slot_hit = (slot_ids == seq_lens[:, None])[:, :, None, None]
        slot_live = (slot_ids <= seq_lens[:, None])[:, None, None, :]
        k_layers = []
        v_layers = []
        for layer_idx in range(layers):
            queries = jnp.dot(hidden, w_query[layer_idx], preferred_element_type=jnp.float32).astype(jnp.bfloat16).reshape(home_rows, kv_heads, group_size, head_dim)
            k_new = jnp.dot(hidden, w_key[layer_idx], preferred_element_type=jnp.float32).astype(jnp.bfloat16).reshape(home_rows, 1, kv_heads, head_dim)
            v_new = jnp.dot(hidden, w_value[layer_idx], preferred_element_type=jnp.float32).astype(jnp.bfloat16).reshape(home_rows, 1, kv_heads, head_dim)
            k_cache = jnp.where(slot_hit, k_new, k_suffix[layer_idx])
            v_cache = jnp.where(slot_hit, v_new, v_suffix[layer_idx])
            k_layers.append(k_cache)
            v_layers.append(v_cache)
            group_queries = lax.all_gather(queries, 'ctx', axis=0, tiled=True)
            pre_scores = jnp.einsum('bkgd,pkd->bkgp', group_queries, k_prefix[layer_idx], preferred_element_type=jnp.float32) * score_scale
            pre_max = pre_scores.max(axis=-1)
            pre_exp = jnp.exp(pre_scores - pre_max[..., None])
            pre_mass = pre_exp.sum(axis=-1)
            pre_vals = jnp.einsum('bkgp,pkd->bkgd', pre_exp.astype(jnp.bfloat16), v_prefix[layer_idx], preferred_element_type=jnp.float32)
            part_out = (pre_vals / pre_mass[..., None]).astype(jnp.bfloat16)
            part_lse = pre_max + jnp.log(pre_mass)
            home_out = lax.all_to_all(part_out, 'ctx', 0, 0, tiled=True).reshape(ctx_size, home_rows, kv_heads, group_size, head_dim)
            home_lse = lax.all_to_all(part_lse, 'ctx', 0, 0, tiled=True).reshape(ctx_size, home_rows, kv_heads, group_size)
            suf_scores = jnp.einsum('bkgd,bskd->bkgs', queries, k_cache, preferred_element_type=jnp.float32) * score_scale
            suf_scores = jnp.where(slot_live, suf_scores, -jnp.inf)
            suf_max = suf_scores.max(axis=-1)
            suf_exp = jnp.exp(suf_scores - suf_max[..., None])
            suf_mass = suf_exp.sum(axis=-1)
            suf_vals = jnp.einsum('bkgs,bskd->bkgd', suf_exp.astype(jnp.bfloat16), v_cache, preferred_element_type=jnp.float32)
            row_max = jnp.maximum(home_lse.max(axis=0), suf_max)
            part_weight = jnp.exp(home_lse - row_max)
            suf_weight = jnp.exp(suf_max - row_max)
            mass_sum = part_weight.sum(axis=0) + suf_weight * suf_mass
            mixed_sum = (part_weight[..., None] * home_out.astype(jnp.float32)).sum(axis=0) + suf_weight[..., None] * suf_vals
            attended = (mixed_sum / mass_sum[..., None]).astype(jnp.bfloat16).reshape(home_rows, num_heads * head_dim)
            update = jnp.dot(attended, w_out[layer_idx], preferred_element_type=jnp.float32).astype(jnp.bfloat16)
            hidden = (hidden.astype(jnp.float32) + update.astype(jnp.float32)).astype(jnp.bfloat16)
        return hidden, jnp.stack(k_layers), jnp.stack(v_layers)

    return jax.shard_map(local_step, mesh=mesh, in_specs=(row_spec, lens_spec, whole_spec, whole_spec, whole_spec, whole_spec, prefix_spec, prefix_spec, cache_spec, cache_spec), out_specs=(row_spec, cache_spec, cache_spec), check_vma=False)
```

profile of v0, /device:TPU:21, one launch (start us, length us, event | category | flops | bytes accessed | tf_op | source)
XLA Modules:
  0.0 279.3 jit_solution(11716336544800968275)
XLA Ops:
  7.3 20.6 %fusion.17 = bf16[32,5120]{1,0:T(8,128)(2,1)S(1)} fusion(bf16[32,5120]{1,0:T(8,128)(2,1)} %param.10, bf16[1,5120,5120]{2,1,0:T(8,128)(2,1)} %param.12), kind=kOutput, calls=%fused_computation.20 | convolution fusion | flops 1677885440 | bytes 53084160 | tf_op jit(solution)/shard_map/dot_general | solution.py:31
  28.3 1.0 copy.45
  29.3 45.4 %all-gather.2.cloned.1.call-done = bf16[512,8,5,128]{3,0,2,1:T(8,128)(2,1)} async-done(((bf16[32,8,5,128]{3,0,2,1:T(8,128)(2,1)}), bf16[512,8,5,128]{3,0,2,1:T(8,128)(2,1)}) %all-gather.2.cloned.1.call-update) | async-done | bytes 5242896 | tf_op jit(solution)/shard_map/all_gather | solution.py:38
  74.7 11.1 %bitcast_reduce_fusion = (f32[512,8,5]{0,2,1:T(8,128)S(1)}, f32[8,512,5,256]{1,3,2,0:T(8,128)}) fusion(bf16[512,8,5,128]{3,0,2,1:T(8,128)(2,1)} %all-gather.2.cloned.1.call-done, bf16[256,8,128,1]{2,1,0,3:T(8,128)(2,1)S(1)} %bitcast.74), kind=kOutput, calls=%fused_computation.5 | convolution fusion | flops 1352642560 | bytes 26820608 | tf_op jit(solution)/shard_map/bkgd,pkd->bkgp/dot_general | solution.py:39
  85.9 9.1 %fusion.6 = f32[512,8,5]{0,2,1:T(8,128)S(1)} fusion(f32[8,512,5,256]{1,3,2,0:T(8,128)} %get-tuple-element.14, f32[512,8,5]{0,2,1:T(8,128)S(1)} %get-tuple-element.13), kind=kLoop, calls=%fused_computation.8 | loop fusion | flops 15708160 | bytes 21135360 | tf_op jit(solution)/shard_map/reduce_sum | solution.py:42
  95.0 0.8 copy.47
  95.7 1.2 reshape.91
  96.9 4.6 %all-to-all-start = ((f32[16,1,1280]{2,1,0:T(1,128)}), f32[16,1,1280]{2,1,0:T(1,128)S(1)}, u32[]{:S(2)}, u32[]{:S(2)}) async-start(f32[16,1,1280]{2,1,0:T(1,128)} %reshape.91), calls=%async_computation | async-start | bytes 163840 | tf_op jit(solution)/shard_map/all_to_all | solution.py:47
  101.5 10.7 %fusion.11 = bf16[512,8,5,128]{3,0,2,1:T(8,128)(2,1)S(1)} fusion(f32[512,8,5]{0,2,1:T(8,128)S(1)} %fusion.6, f32[8,512,5,256]{1,3,2,0:T(8,128)} %get-tuple-element.14, f32[512,8,5]{0,2,1:T(8,128)S(1)} %get-tuple-element.13, bf16[256,8,128,1]{2,1,0,3:T(8,128)(2,1)} %bitcast.82), kind=kOutput, calls=%fused_computation.13 | convolution fusion | flops 1363148800 | bytes 26902528 | tf_op jit(solution)/shard_map/bkgp,pkd->bkgd/dot_general | solution.py:43
  112.2 5.7 %copy.54 = bf16[512,8,5,128]{3,1,2,0:T(8,128)(2,1)} copy(bf16[512,8,5,128]{3,0,2,1:T(8,128)(2,1)S(1)} %fusion.11) | data formatting | bytes 10485760 | tf_op jit(solution)/shard_map/convert_element_type | solution.py:44
  117.9 7.2 %all-to-all-start.1 = ((bf16[512,8,5,128]{3,1,2,0:T(8,128)(2,1)}), bf16[512,8,5,128]{3,1,2,0:T(8,128)(2,1)}, u32[]{:S(2)}, u32[]{:S(2)}) async-start(bf16[512,8,5,128]{3,1,2,0:T(8,128)(2,1)} %copy.54), calls=%async_computation.1 | async-start | bytes 10485760 | tf_op jit(solution)/shard_map/all_to_all | solution.py:46
  125.1 5.9 %fusion.65 = bf16[4,8,8,128]{3,1,2,0:T(8,128)(2,1)S(1)} fusion(bf16[32,5120]{1,0:T(8,128)(2,1)S(1)} %copy-done.2, bf16[1,5120,1024]{2,1,0:T(8,128)(2,1)} %param.13), kind=kOutput, calls=%fused_computation.42 | convolution fusion | flops 335577088 | bytes 10878976 | tf_op jit(solution)/shard_map/dot_general | solution.py:32
  131.1 6.0 %fusion.62 = bf16[4,8,8,128]{3,1,2,0:T(8,128)(2,1)S(1)} fusion(bf16[32,5120]{1,0:T(8,128)(2,1)S(1)} %copy-done.2, bf16[1,5120,1024]{2,1,0:T(8,128)(2,1)} %param.14), kind=kOutput, calls=%fused_computation.41 | convolution fusion | flops 335577088 | bytes 10878976 | tf_op jit(solution)/shard_map/dot_general | solution.py:33
  137.2 2.7 bitcast_select_fusion.1
  139.9 2.3 fusion.77
  142.3 1.9 fusion.68
  144.3 4.7 %broadcast_select_fusion = (bf16[1,32,32,8,128]{4,3,2,1,0:T(8,128)(2,1)}, bf16[1,32,32,8,128]{4,3,2,1,0:T(8,128)(2,1)}) fusion(bf16[1,32,32,8,128]{4,3,2,1,0:T(8,128)(2,1)} %param.19, pred[32,32]{1,0:T(8,128)(4,1)S(1)} %get-tuple-element.12, bf16[32,8,128]{2,1,0:T(8,128)(2,1)S(1)} %bitcast.81, bf16[1,32,32,8,128]{4,3,2,1,0:T(8,128)(2,1)S(1)} %copy-done.3, ...), kind=kLoop, calls=%fused_computation.31 | loop fusion | flops 2097152 | bytes 8520704 | tf_op jit(solution)/shard_map/jit(_where)/select_n | solution.py:35
  149.6 0.8 reduce
  150.4 0.6 reshape.92
  152.3 89.8 %all-to-all-done.1 = bf16[512,8,5,128]{3,1,2,0:T(8,128)(2,1)} async-done(((bf16[512,8,5,128]{3,1,2,0:T(8,128)(2,1)}), bf16[512,8,5,128]{3,1,2,0:T(8,128)(2,1)}, u32[]{:S(2)}, u32[]{:S(2)}) %all-to-all-start.1) | async-done | bytes 5242912 | tf_op jit(solution)/shard_map/all_to_all | solution.py:46
  242.1 3.7 %bitcast_convert_fusion = f32[16,32,8,5,128]{4,2,3,1,0:T(8,128)S(1)} fusion(bf16[512,8,5,128]{3,1,2,0:T(8,128)(2,1)} %all-to-all-done.1), kind=kLoop, calls=%fused_computation.56 | loop fusion | flops 2621440 | bytes 15728640 | tf_op jit(solution)/shard_map/convert_element_type | solution.py:58
  245.9 2.8 fusion.14
  248.7 1.6 fusion.53
  250.7 21.7 %fusion.29 = bf16[32,5120]{1,0:T(8,128)(2,1)} fusion(bf16[32,5120]{1,0:T(8,128)(2,1)S(1)} %reshape.87, bf16[1,5120,5120]{2,1,0:T(8,128)(2,1)} %param.15, bf16[32,5120]{1,0:T(8,128)(2,1)S(1)} %copy-done.2), kind=kOutput, calls=%fused_computation.24 | convolution fusion | flops 1678540800 | bytes 53411840 | tf_op jit(solution)/shard_map/dot_general | solution.py:60
  (36 shorter events, 3.1 us)
Async XLA Ops:
  7.2 67.6 %copy-start = (bf16[1,256,8,128]{3,2,1,0:T(8,128)(2,1)S(1)}, bf16[1,256,8,128]{3,2,1,0:T(8,128)(2,1)}, u32[]{:S(2)}) copy-start(bf16[1,256,8,128]{3,2,1,0:T(8,128)(2,1)} %param.16) | copy-start | bytes 1572868
  7.2 67.5 %all-gather.2.cloned.1.call-start = ((), (), s32[]{:S(2)}) async-start(), calls=%async_computation.2 | async-start | bytes 5570560 | tf_op jit(solution)/shard_map/all_gather | solution.py:38
  96.9 21.0 %all-to-all-start = ((f32[16,1,1280]{2,1,0:T(1,128)}), f32[16,1,1280]{2,1,0:T(1,128)S(1)}, u32[]{:S(2)}, u32[]{:S(2)}) async-start(f32[16,1,1280]{2,1,0:T(1,128)} %reshape.91), calls=%async_computation | async-start | bytes 163840 | tf_op jit(solution)/shard_map/all_to_all | solution.py:47
  112.2 13.0 %copy-start.2 = (bf16[32,5120]{1,0:T(8,128)(2,1)S(1)}, bf16[32,5120]{1,0:T(8,128)(2,1)}, u32[]{:S(2)}) copy-start(bf16[32,5120]{1,0:T(8,128)(2,1)} %param.10) | copy-start | bytes 983044
  117.9 124.2 %all-to-all-start.1 = ((bf16[512,8,5,128]{3,1,2,0:T(8,128)(2,1)}), bf16[512,8,5,128]{3,1,2,0:T(8,128)(2,1)}, u32[]{:S(2)}, u32[]{:S(2)}) async-start(bf16[512,8,5,128]{3,1,2,0:T(8,128)(2,1)} %copy.54), calls=%async_computation.1 | async-start | bytes 10485760 | tf_op jit(solution)/shard_map/all_to_all | solution.py:46
  131.0 6.1 %copy-start.7 = (s32[32]{0:T(128)S(1)}, s32[32]{0:T(128)}, u32[]{:S(2)}) copy-start(s32[32]{0:T(128)} %param.11) | copy-start | bytes 388
  131.0 6.2 %copy-start.3 = (bf16[1,32,32,8,128]{4,3,2,1,0:T(8,128)(2,1)S(1)}, bf16[1,32,32,8,128]{4,3,2,1,0:T(8,128)(2,1)}, u32[]{:S(2)}) copy-start(bf16[1,32,32,8,128]{4,3,2,1,0:T(8,128)(2,1)} %param.18) | copy-start | bytes 6291460
  131.1 6.2 %copy-start.4 = (bf16[1,32,32,8,128]{4,3,2,1,0:T(8,128)(2,1)S(1)}, bf16[1,32,32,8,128]{4,3,2,1,0:T(8,128)(2,1)}, u32[]{:S(2)}) copy-start(bf16[1,32,32,8,128]{4,3,2,1,0:T(8,128)(2,1)} %param.19) | copy-start | bytes 6291460
  152.3 96.3 %copy-start.5 = (f32[32,8,5,32]{3,2,1,0:T(8,128)S(1)}, f32[32,8,5,32]{3,2,1,0:T(8,128)}, u32[]{:S(2)}) copy-start(f32[32,8,5,32]{3,2,1,0:T(8,128)} %get-tuple-element.16) | copy-start | bytes 491524
  242.1 6.5 %copy-start.6 = (bf16[32,32,8,128]{3,2,1,0:T(8,128)(2,1)S(1)}, bf16[32,32,8,128]{3,2,1,0:T(8,128)(2,1)}, u32[]{:S(2)}) copy-start(bf16[32,32,8,128]{3,2,1,0:T(8,128)(2,1)} %get-tuple-element.10) | copy-start | bytes 6291460
  250.7 21.7 %copy-start.1 = (bf16[1,256,8,128]{3,2,1,0:T(8,128)(2,1)S(1)}, bf16[1,256,8,128]{3,2,1,0:T(8,128)(2,1)}, u32[]{:S(2)}) copy-start(bf16[1,256,8,128]{3,2,1,0:T(8,128)(2,1)} %param.16) | copy-start | bytes 1572868
Sparse Core Ops, SparseCore 0:
  29.5 45.2 all-gather.1
where the time goes:
time: 280 us; the launch traced here: 279 us
  waiting for transfers between devices  135 us (48%)
  matrix products  79.9 us (29%)
  other arithmetic  26.2 us (9%)
  between operations  14.3 us (5%)
  starting transfers between devices  11.9 us (4%)
  local copies, waits for them, and re-layouts  11.8 us (4%)
    all_to_all x1, waiting for transfers between devices, local_step(): lax.all_to_all(part_out, 'ctx', 0, 0, tiled=True)  89.8 us
    all_gather x1, waiting for transfers between devices, local_step(): group_queries = lax.all_gather(queries, 'ctx', axis=0, tiled=True)  45.4 us
    dot_general x1, matrix products, local_step(): jnp.dot(attended, w_out[layer_idx], preferred_element_type=jnp.float32)  21.7 us
    dot_general x1, matrix products, local_step(): jnp.dot(hidden, w_query[layer_idx], preferred_element_type=jnp.float32)  20.6 us
    dot_general x1, matrix products, local_step(): jnp.einsum('bkgd,pkd->bkgp', group_queries, k_prefix[layer_idx], preferre...  11.1 us
    dot_general x1, matrix products, local_step(): jnp.einsum('bkgp,pkd->bkgd', pre_exp.astype(jnp.bfloat16), v_prefix[layer...  10.7 us
    reduce_sum x1, other arithmetic, local_step(): pre_mass = pre_exp.sum(axis=-1)  9.05 us
    all_to_all x1, starting transfers between devices, local_step(): lax.all_to_all(part_out, 'ctx', 0, 0, tiled=True)  7.24 us
  transfers between devices with their start and end apart: 3, of which 2 were waited for; matrix products, arithmetic and copies ran while one was open for 16% of the time, Pallas kernels for 0%

commit v1 on v0

v1 whole, which is shorter than its diff:
```python
import functools
import math

import jax
import jax.numpy as jnp
from jax import lax
from jax.experimental import pallas as pl
from jax.experimental.pallas import tpu as pltpu
from jax.sharding import PartitionSpec as P

MESH = pl.DeviceIdType.MESH
CORES = 2
CHUNK = 512
RING = 3
OUT_SLOTS = 5
UNROLL = 4


def hop_of(step):
    return (step + 1) // 2 * (1 - 2 * ((step + 1) % 2))


def decode_kernel(n, dims, lens, x_hbm, wq, wk, wv, wo, kp, vp, ks_hbm, vs_hbm, out_ref, kn_out,
                  x2, wqb, wkb, wvb, wob, kraw, vraw, tmp, kvsend, kvrecv, acc, qsend, qrecv, qsib, knv_send, knv_recv,
                  q32, kn32, vn32, ksuf, vsuf, suf_o, suf_m, suf_l, scr, osend, lsend, orecv, lrecv, oacc,
                  in_sem, wsem, wosem, x_ssem, x_rsem, kv_ssem, kv_rsem, fw_ssem, q_ssem, q_rsem, sib_ssem, sib_rsem,
                  o_ssem, o_rsem, l_ssem, l_rsem):
    rows, model, heads, group, dim, slots, pre = dims
    chips = n // CORES
    qw = heads * group * dim
    q_half = qw // CORES
    kv_half = heads * dim // CORES
    my_heads = heads // CORES
    qrows = group * rows
    base2 = dim ** -0.5 * math.log2(math.e)
    me = lax.axis_index('ctx')
    chip = me // CORES
    core = me % CORES
    sib = me + 1 - 2 * core
    f32, bf16 = jnp.float32, jnp.bfloat16
    steps = model // CHUNK
    out_rows = qw // chips

    def loads():
        return [
            pltpu.make_async_copy(kp, kraw, in_sem.at[0]),
            pltpu.make_async_copy(vp, vraw, in_sem.at[1]),
            pltpu.make_async_copy(x_hbm, x2.at[core], in_sem.at[2]),
            pltpu.make_async_copy(ks_hbm, ksuf, in_sem.at[3]),
            pltpu.make_async_copy(vs_hbm, vsuf, in_sem.at[4]),
        ]

    def weight_copies(step, slot):
        r = pl.ds(pl.multiple_of(step * CHUNK, CHUNK), CHUNK)
        qc = pl.ds(pl.multiple_of(core * q_half, 128), q_half)
        kc = pl.ds(pl.multiple_of(core * kv_half, 128), kv_half)
        return [
            pltpu.make_async_copy(wq.at[0, r, qc], wqb.at[slot], wsem.at[slot, 0]),
            pltpu.make_async_copy(wk.at[0, r, kc], wkb.at[slot], wsem.at[slot, 1]),
            pltpu.make_async_copy(wv.at[0, r, kc], wvb.at[slot], wsem.at[slot, 2]),
        ]

    def home_of(step):
        return lax.rem(chip + hop_of(step) + chips, chips)

    def head_of(step):
        return lax.rem(chip - hop_of(step) + chips, chips)

    def out_copy(step):
        slot = lax.rem(step, OUT_SLOTS)
        r = pl.ds(pl.multiple_of(head_of(step) * out_rows, out_rows), out_rows)
        return pltpu.make_async_copy(wo.at[0, r, :], wob.at[slot], wosem.at[slot])

    first = loads()
    for c in first[:3]:
        c.start()
    for s in range(RING):
        for c in weight_copies(s, s):
            c.start()

    barrier = pltpu.get_barrier_semaphore()

    @pl.loop(1, n)
    def _(d):
        pl.semaphore_signal(barrier, inc=1, device_id={'ctx': lax.rem(me + d, n)}, device_id_type=MESH)

    for c in first[3:]:
        c.start()
    for part, raw in ((0, kraw), (1, vraw)):
        first[part].wait()
        tmp[...] = raw[...].astype(f32)
        for h in range(heads):
            kvsend[h, part] = tmp[pl.ds(h, pre, stride=heads), :].astype(bf16)
    kvrecv[me] = kvsend[chip]
    acc[...] = jnp.zeros_like(acc)
    first[2].wait()
    pl.semaphore_wait(barrier, n - 1)

    x_copy = pltpu.make_async_remote_copy(x2.at[core], x2.at[core], x_ssem, x_rsem, device_id={'ctx': sib}, device_id_type=MESH)
    x_copy.start()

    def kv_copy(step):
        t = home_of(step)
        return pltpu.make_async_remote_copy(kvsend.at[t], kvrecv.at[me], kv_ssem.at[step], kv_rsem.at[me],
                                            device_id={'ctx': t * CORES + core}, device_id_type=MESH)

    def fw_copy(step):
        j = home_of(step) * CORES + core
        src = kvsend.at[chip] if step == 0 else kvrecv.at[j]
        return pltpu.make_async_remote_copy(src, kvrecv.at[j], fw_ssem.at[step], kv_rsem.at[j],
                                            device_id={'ctx': sib}, device_id_type=MESH)

    def kv_arrival(j):
        return pltpu.make_async_remote_copy(kvsend.at[0], kvrecv.at[j], kv_ssem.at[0], kv_rsem.at[j],
                                            device_id={'ctx': sib}, device_id_type=MESH)

    for step in range(1, chips):
        kv_copy(step).start()
    fw_copy(0).start()
    x_copy.wait()

    @pl.loop(0, steps)
    def _(j):
        slot = lax.rem(j, RING)
        for c in weight_copies(j, slot):
            c.wait()
        xc = x2[:, :, pl.ds(pl.multiple_of(j * CHUNK, CHUNK), CHUNK)].reshape(CORES * rows, CHUNK)
        for b in range(0, q_half, 512):
            acc[:, b:b + 512] += jnp.dot(xc, wqb[slot, :, b:b + 512], preferred_element_type=f32)
        acc[:, q_half:q_half + kv_half] += jnp.dot(xc, wkb[slot], preferred_element_type=f32)
        acc[:, q_half + kv_half:] += jnp.dot(xc, wvb[slot], preferred_element_type=f32)

        @pl.when(j + RING < steps)
        def _():
            for c in weight_copies(j + RING, slot):
                c.start()

        @pl.when(j + RING >= steps)
        def _():
            out_copy(j + RING - steps).start()

    for s in range(RING, OUT_SLOTS):
        out_copy(s).start()

    for hh in range(my_heads * group):
        tl, g = hh // group, hh % group
        block = acc[:, hh * dim:(hh + 1) * dim].astype(bf16)
        for r in range(CORES):
            qsend[r, tl, g * rows:(g + 1) * rows, :] = block[r * rows:(r + 1) * rows]
    for part in range(2):
        for hl in range(my_heads):
            lo = q_half + part * kv_half + hl * dim
            block = acc[:, lo:lo + dim].astype(bf16)
            for r in range(CORES):
                knv_send[r, part, hl * rows:(hl + 1) * rows, :] = block[r * rows:(r + 1) * rows]

    def sib_copies():
        return [
            pltpu.make_async_remote_copy(qsend.at[1 - core], qsib, sib_ssem.at[0], sib_rsem.at[0], device_id={'ctx': sib}, device_id_type=MESH),
            pltpu.make_async_remote_copy(knv_send.at[1 - core], knv_recv, sib_ssem.at[1], sib_rsem.at[1], device_id={'ctx': sib}, device_id_type=MESH),
        ]

    for c in sib_copies():
        c.start()

    def q_copy(tl, r):
        t = core * my_heads + tl
        return pltpu.make_async_remote_copy(qsend.at[r, tl], qrecv.at[chip], q_ssem.at[tl, r], q_rsem.at[chip],
                                            device_id={'ctx': t * CORES + r}, device_id_type=MESH)

    def q_arrival(c):
        return pltpu.make_async_remote_copy(qsend.at[0, 0], qrecv.at[c], q_ssem.at[0, 0], q_rsem.at[c],
                                            device_id={'ctx': sib}, device_id_type=MESH)

    q_is_local = chip // my_heads == core

    @pl.loop(0, my_heads)
    def _(i):
        tl = lax.rem(chip + i, my_heads)
        for r in range(CORES):
            here = jnp.logical_and(core * my_heads + tl == chip, core == r)

            @pl.when(jnp.logical_not(here))
            def _():
                q_copy(tl, r).start()

            @pl.when(here)
            def _():
                qrecv[chip] = qsend[r, tl]

    own = qsend[core].reshape(my_heads * qrows, dim).astype(f32)
    q32[pl.ds(pl.multiple_of(core * my_heads * qrows, 8), my_heads * qrows), :] = own
    own_kv = knv_send[core].astype(f32)
    own_at = pl.ds(pl.multiple_of(core * my_heads * rows, 8), my_heads * rows)
    kn32[own_at, :] = own_kv[0]
    vn32[own_at, :] = own_kv[1]
    for c in sib_copies():
        c.wait()
    sib_at = 1 - core
    q32[pl.ds(pl.multiple_of(sib_at * my_heads * qrows, 8), my_heads * qrows), :] = qsib[...].reshape(my_heads * qrows, dim).astype(f32)
    sib_kv = knv_recv[...].astype(f32)
    other = pl.ds(pl.multiple_of(sib_at * my_heads * rows, 8), my_heads * rows)
    kn32[other, :] = sib_kv[0]
    vn32[other, :] = sib_kv[1]
    kn_out[0] = kn32[...].astype(bf16)
    kn_out[1] = vn32[...].astype(bf16)

    first[3].wait()
    first[4].wait()
    n_q = heads * group
    row_id = lax.broadcasted_iota(jnp.int32, (n_q, slots * heads), 0)
    col_id = lax.broadcasted_iota(jnp.int32, (n_q, slots * heads), 1)
    low = (col_id & (heads - 1)) * group
    same_head = jnp.logical_and(row_id >= low, row_id < low + group)
    slot_of = col_id >> int(math.log2(heads))
    slot3 = lax.broadcasted_iota(jnp.int32, (slots, heads, dim), 0)

    @pl.loop(0, rows // UNROLL)
    def _(i):
        for u in range(UNROLL):
            b = i * UNROLL + u
            length = lens[b]
            qb = q32[pl.ds(b, n_q, stride=rows), :].astype(bf16)
            hit = slot3 == length
            kb = jnp.where(hit, kn32[pl.ds(b, heads, stride=rows), :][None], ksuf[b].astype(f32).reshape(slots, heads, dim))
            vb = jnp.where(hit, vn32[pl.ds(b, heads, stride=rows), :][None], vsuf[b].astype(f32).reshape(slots, heads, dim))
            kb = kb.reshape(slots * heads, dim).astype(bf16)
            vb = vb.reshape(slots * heads, dim).astype(bf16)
            s = lax.dot_general(qb, kb, (((1,), (1,)), ((), ())), preferred_element_type=f32)
            live = jnp.logical_and(same_head, slot_of <= length)
            s = jnp.where(live, s, -jnp.inf)
            m = s.max(axis=-1, keepdims=True)
            p = jnp.where(live, jnp.exp2((s - m) * base2), 0.0)
            l = p.sum(axis=-1, keepdims=True)
            ob = jnp.dot(p.astype(bf16), vb, preferred_element_type=f32)
            at = pl.ds(b, n_q, stride=rows)
            suf_o[at, :] = ob
            suf_m[at, :] = jnp.broadcast_to(m * base2, (n_q, dim))
            suf_l[at, :] = jnp.broadcast_to(l, (n_q, dim))

    for step in range(1, chips):
        kv_arrival(home_of(step) * CORES + core).wait_recv()
        fw_copy(step).start()
    for c in range(chips):
        kv_arrival(c * CORES + 1 - core).wait_recv()

    eye = lax.broadcasted_iota(jnp.int32, (128, 128), 0) == lax.broadcasted_iota(jnp.int32, (128, 128), 1)

    def o_copy(c):
        return pltpu.make_async_remote_copy(osend.at[c], orecv.at[chip], o_ssem.at[c], o_rsem.at[chip],
                                            device_id={'ctx': c * CORES + core}, device_id_type=MESH)

    def l_copy(c):
        return pltpu.make_async_remote_copy(lsend.at[c], lrecv.at[chip], l_ssem.at[c], l_rsem.at[chip],
                                            device_id={'ctx': c * CORES + core}, device_id_type=MESH)

    def o_arrival(t):
        return pltpu.make_async_remote_copy(osend.at[0], orecv.at[t], o_ssem.at[0], o_rsem.at[t],
                                            device_id={'ctx': sib}, device_id_type=MESH)

    def l_arrival(t):
        return pltpu.make_async_remote_copy(lsend.at[0], lrecv.at[t], l_ssem.at[0], l_rsem.at[t],
                                            device_id={'ctx': sib}, device_id_type=MESH)

    @pl.loop(0, chips)
    def _(step):
        c = home_of(step)

        @pl.when(jnp.logical_not(jnp.logical_and(step == 0, q_is_local)))
        def _():
            q_arrival(c).wait_recv()

        q = qrecv[c]
        top = jnp.full((qrows, dim), -jnp.inf, f32)
        for s in range(n):
            sc = lax.dot_general(q, kvrecv[s, 0], (((1,), (1,)), ((), ())), preferred_element_type=f32)
            scr[s] = sc
            for b in range(0, pre, dim):
                top = jnp.maximum(top, sc[:, b:b + dim])
        m = top.max(axis=-1, keepdims=True) * base2
        mass = jnp.zeros((qrows, dim), f32)
        o = jnp.zeros((qrows, dim), f32)
        for s in range(n):
            p = jnp.exp2(scr[s] * base2 - m)
            for b in range(0, pre, dim):
                mass += p[:, b:b + dim]
            o += jnp.dot(p.astype(bf16), kvrecv[s, 1], preferred_element_type=f32)
        l = mass.sum(axis=-1, keepdims=True)
        o = (o / l).astype(bf16)
        lse = jnp.broadcast_to(m + jnp.log2(l), (qrows, dim))
        row0 = jnp.where(eye, lse[:dim], 0.0).sum(axis=0, keepdims=True)
        row1 = jnp.where(eye[:qrows - dim], lse[dim:], 0.0).sum(axis=0, keepdims=True)

        @pl.when(step == 0)
        def _():
            orecv[c] = o
            lrecv[c, 0:1, :] = row0
            lrecv[c, 1:2, :] = row1

        @pl.when(step > 0)
        def _():
            osend[c] = o
            lsend[c] = jnp.zeros_like(lsend[c])
            lsend[c, 0:1, :] = row0
            lsend[c, 1:2, :] = row1
            o_copy(c).start()
            l_copy(c).start()

    oacc[...] = jnp.zeros_like(oacc)

    @pl.loop(0, chips)
    def _(step):
        t = head_of(step)

        @pl.when(step > 0)
        def _():
            o_arrival(t).wait_recv()
            l_arrival(t).wait_recv()

        row0 = jnp.broadcast_to(lrecv[t, 0:1, :], (dim, dim))
        row1 = jnp.broadcast_to(lrecv[t, 1:2, :], (qrows - dim, dim))
        lse = jnp.concatenate([
            jnp.where(eye, row0, 0.0).sum(axis=-1, keepdims=True),
            jnp.where(eye[:qrows - dim], row1, 0.0).sum(axis=-1, keepdims=True),
        ], axis=0)
        at = pl.ds(pl.multiple_of(t * qrows, 8), qrows)
        sm = suf_m[at, :]
        top = jnp.maximum(lse, sm)
        wp = jnp.exp2(lse - top)
        ws = jnp.exp2(sm - top)
        o = (wp * orecv[t].astype(f32) + ws * suf_o[at, :]) / (wp + ws * suf_l[at, :])
        o = o.astype(bf16)
        att = jnp.concatenate([o[g * rows:(g + 1) * rows] for g in range(group)], axis=1)
        out_copy(step).wait()
        slot = lax.rem(step, OUT_SLOTS)
        for b in range(0, model, 512):
            oacc[:, b:b + 512] += jnp.dot(att, wob[slot, :, b:b + 512], preferred_element_type=f32)

        @pl.when(step + OUT_SLOTS < chips)
        def _():
            out_copy(step + OUT_SLOTS).start()

    out_ref[...] = (x2[core].astype(f32) + oacc[...].astype(bf16).astype(f32)).astype(bf16)

    for step in range(1, chips):
        kv_copy(step).wait_send()
    for step in range(chips):
        fw_copy(step).wait_send()

    @pl.loop(0, my_heads)
    def _(tl):
        for r in range(CORES):
            @pl.when(jnp.logical_not(jnp.logical_and(core * my_heads + tl == chip, core == r)))
            def _():
                q_copy(tl, r).wait_send()

    @pl.loop(1, chips)
    def _(step):
        c = home_of(step)
        o_copy(c).wait_send()
        l_copy(c).wait_send()


def solution(mesh):
    n = mesh.shape['ctx']
    home_axes = ('data', 'ctx')
    row_spec = P(home_axes, None)
    lens_spec = P(home_axes)
    whole_spec = P()
    prefix_spec = P(None, home_axes, None, None)
    cache_spec = P(None, home_axes, None, None, None)
    bf16, f32 = jnp.bfloat16, jnp.float32

    def attend(hidden, seq_lens, wq, wk, wv, wo, kp, vp, ks, vs):
        rows, model = hidden.shape
        _, pre, heads, dim = kp.shape
        slots = ks.shape[2]
        group = wq.shape[2] // (heads * dim)
        chips = n // CORES
        my_heads = heads // CORES
        qrows = group * rows
        qw = heads * group * dim
        dims = (rows, model, heads, group, dim, slots, pre)
        dma = pltpu.SemaphoreType.DMA
        vmem = pltpu.VMEM
        scratch = [
            vmem((CORES, rows, model), bf16),
            vmem((RING, CHUNK, qw // CORES), bf16),
            vmem((RING, CHUNK, heads * dim // CORES), bf16),
            vmem((RING, CHUNK, heads * dim // CORES), bf16),
            vmem((OUT_SLOTS, qw // chips, model), bf16),
            vmem((pre * heads, dim), bf16),
            vmem((pre * heads, dim), bf16),
            vmem((pre * heads, dim), f32),
            vmem((heads, 2, pre, dim), bf16),
            vmem((n, 2, pre, dim), bf16),
            vmem((CORES * rows, (qw + 2 * heads * dim) // CORES), f32),
            vmem((CORES, my_heads, qrows, dim), bf16),
            vmem((chips, qrows, dim), bf16),
            vmem((my_heads, qrows, dim), bf16),
            vmem((CORES, 2, my_heads * rows, dim), bf16),
            vmem((2, my_heads * rows, dim), bf16),
            vmem((heads * qrows, dim), f32),
            vmem((heads * rows, dim), f32),
            vmem((heads * rows, dim), f32),
            vmem((rows, slots * heads, dim), bf16),
            vmem((rows, slots * heads, dim), bf16),
            vmem((heads * qrows, dim), f32),
            vmem((heads * qrows, dim), f32),
            vmem((heads * qrows, dim), f32),
            vmem((n, qrows, pre), f32),
            vmem((chips, qrows, dim), bf16),
            vmem((chips, 8, dim), f32),
            vmem((chips, qrows, dim), bf16),
            vmem((chips, 8, dim), f32),
            vmem((rows, model), f32),
            dma((5,)),
            dma((RING, 3)),
            dma((OUT_SLOTS,)),
            dma,
            dma,
            dma((chips,)),
            dma((n,)),
            dma((chips,)),
            dma((my_heads, CORES)),
            dma((chips,)),
            dma((2,)),
            dma((2,)),
            dma((chips,)),
            dma((chips,)),
            dma((chips,)),
            dma((chips,)),
        ]
        any_spec = pl.BlockSpec(memory_space=pl.ANY)
        vmem_spec = pl.BlockSpec(memory_space=pltpu.VMEM)
        return pl.pallas_call(
            functools.partial(decode_kernel, n, dims),
            out_shape=(jax.ShapeDtypeStruct((rows, model), bf16), jax.ShapeDtypeStruct((2, heads * rows, dim), bf16)),
            in_specs=[pl.BlockSpec(memory_space=pltpu.SMEM)] + [any_spec] * 9,
            out_specs=(vmem_spec, vmem_spec),
            scratch_shapes=scratch,
            compiler_params=pltpu.CompilerParams(collective_id=0, has_side_effects=True, vmem_limit_bytes=67_043_328),
        )(seq_lens, hidden, wq, wk, wv, wo, kp.reshape(pre * heads, dim), vp.reshape(pre * heads, dim),
          ks.reshape(rows, slots * heads, dim), vs.reshape(rows, slots * heads, dim))

    def local_step(hidden, seq_lens, wq, wk, wv, wo, kp, vp, ks, vs):
        rows = hidden.shape[0]
        _, _, slots, heads, dim = ks.shape
        out, new = attend(hidden, seq_lens, wq, wk, wv, wo, kp, vp, ks, vs)
        hit = (lax.broadcasted_iota(jnp.int32, (rows, slots), 1) == seq_lens[:, None])[None, :, :, None, None]
        new = new.reshape(2, heads, rows, dim).transpose(0, 2, 1, 3)[:, None, :, None]
        return out, jnp.where(hit, new[0], ks), jnp.where(hit, new[1], vs)

    return jax.shard_map(local_step, mesh=mesh, in_specs=(row_spec, lens_spec, whole_spec, whole_spec, whole_spec, whole_spec, prefix_spec, prefix_spec, cache_spec, cache_spec), out_specs=(row_spec, cache_spec, cache_spec), check_vma=False)
```

time: 280 us -> 74.2 us (0.27)
  waiting for transfers between devices: 135 us -> 0 us
  matrix products: 79.9 us -> 0 us
  Pallas kernels: 0 us -> 65 us
  other arithmetic: 26.2 us -> 6.6 us
  between operations: 14.3 us -> 0.66 us
  starting transfers between devices: 11.9 us -> 0 us
  local copies, waits for them, and re-layouts: 11.8 us -> 1.67 us
    all_to_all x2 -> x0, waiting for transfers between devices: 89.8 us -> none  [the longest x1 89.8 us: local_step(): lax.all_to_all(part_out, 'ctx', 0, 0, tiled=True)]
    dot_general x8 -> x0, matrix products: 79.9 us -> none  [the longest x1 21.7 us: local_step(): jnp.dot(attended, w_out[layer_idx], preferred_element_type=jnp.float32)]
    pallas_call x0 -> x1, Pallas kernels: none -> 65 us  [attend(): pl.pallas_call(functools.partial(decode_kernel, n, dims), out_shape=(jax....]
    all_gather x1 -> x0, waiting for transfers between devices: 45.4 us -> none  [local_step(): group_queries = lax.all_gather(queries, 'ctx', axis=0, tiled=True)]
    reduce_sum x4 -> x0, other arithmetic: 13.8 us -> none  [the longest x1 9.05 us: local_step(): pre_mass = pre_exp.sum(axis=-1)]
    all_to_all x2 -> x0, starting transfers between devices: 11.9 us -> none  [the longest x1 7.24 us: local_step(): lax.all_to_all(part_out, 'ctx', 0, 0, tiled=True)]
    convert_element_type x1 -> x0, local copies, waits for them, and re-layouts: 5.72 us -> none  [local_step(): part_out = (pre_vals / pre_mass[..., None]).astype(jnp.bfloat16)]
    convert_element_type x1 -> x0, other arithmetic: 3.74 us -> none  [local_step(): home_out.astype(jnp.float32)]
  transfers between devices with their start and end apart: 3 -> 0, of which waited for: 2 -> 0; matrix products, arithmetic and copies ran while one was open for 16% -> 0% of each run, Pallas kernels for 0% -> 0%
where the time goes in v1:
time: 74.2 us; the launch traced here: 74 us
  Pallas kernels  65 us (88%)
  other arithmetic  6.6 us (9%)
  local copies, waits for them, and re-layouts  1.67 us (2%)
    pallas_call x1, Pallas kernels, attend(): pl.pallas_call(functools.partial(decode_kernel, n, dims), out_shape=(jax....  65 us
    select_n x1, other arithmetic, local_step(): return (out, jnp.where(hit, new[0], ks), jnp.where(hit, new[1], vs))  5.28 us

profile of v1, /device:TPU:21, one launch (start us, length us, event | category | flops | bytes accessed | tf_op | source)
XLA Modules:
  0.0 74.0 jit_solution(13546423392675495623)
XLA Ops:
  0.6 1.3 %iota_compare_fusion = pred[32,32]{1,0:T(8,128)(4,1)} fusion(s32[32]{0:T(128)} %lens.1), kind=kLoop, calls=%fused_computation.4 | loop fusion | flops 1024 | bytes 1152 | tf_op jit(solution)/shard_map/eq | solution.py:450
  2.0 65.0 %shard_map.121 = (bf16[32,5120]{1,0:T(8,128)(2,1)}, bf16[2,256,128]{2,1,0:T(8,128)(2,1)}) custom-call(s32[32]{0:T(128)} %lens.1, bf16[32,5120]{1,0:T(8,128)(2,1)} %x_hbm.1, bf16[1,5120,5120]{2,1,0:T(8,128)(2,1)} %wq.1, bf16[1,5120,1024]{2,1,0:T(8,128)(2,1)} %wk.1, bf16[1,5120,1024]{2,1,0:T(8,128)(2,1)} %wv.1, bf16[1,5120,5120]{2,1,0:T(8,128)(2,1)} %wo.1, ...), custom_call_target="tpu_custom_call" | custom-call | tf_op jit(solution)/shard_map/pallas_call | solution.py:436
  67.0 0.9 %slice_bitcast_fusion = (bf16[32,8,128]{2,0,1:T(8,128)(2,1)S(1)}, bf16[32,8,128]{2,0,1:T(8,128)(2,1)S(1)}) fusion(bf16[2,32,8,128]{3,1,2,0:T(8,128)(2,1)} %bitcast.15), kind=kLoop, calls=%fused_computation.2 | loop fusion | bytes 262144 | tf_op jit(solution)/shard_map/jit(_where)/broadcast_in_dim | solution.py:452
  67.9 0.0 copy-start
  67.9 5.3 %broadcast_select_fusion = (bf16[1,32,32,8,128]{4,3,2,1,0:T(8,128)(2,1)}, bf16[1,32,32,8,128]{4,3,2,1,0:T(8,128)(2,1)}) fusion(bf16[1,32,32,8,128]{4,3,2,1,0:T(8,128)(2,1)} %param.19, pred[32,32]{1,0:T(8,128)(4,1)} %iota_compare_fusion, bf16[32,8,128]{2,1,0:T(8,128)(2,1)S(1)} %copy.14, bf16[1,32,32,8,128]{4,3,2,1,0:T(8,128)(2,1)} %param.18, ...), kind=kLoop, calls=%fused_computation | loop fusion | flops 2097152 | bytes 8520704 | tf_op jit(solution)/shard_map/jit(_where)/select_n | solution.py:452
  73.2 0.0 copy-done
  73.2 0.7 copy.16
  (2 shorter events, 0.1 us)
Async XLA Ops:
  67.9 5.3 %copy-start = (bf16[32,5120]{1,0:T(8,128)(2,1)S(1)}, bf16[32,5120]{1,0:T(8,128)(2,1)}, u32[]{:S(2)}) copy-start(bf16[32,5120]{1,0:T(8,128)(2,1)} %get-tuple-element.14) | copy-start | bytes 983044

commit v2 on v1

--- a/solution.py
+++ b/solution.py
@@ -12,7 +12,9 @@
 CORES = 2
 CHUNK = 512
 RING = 3
-OUT_SLOTS = 5
+OUT_SLOTS = 4
+TILE = 256
+HOME_AFTER = {2: (0, 1), 3: (1, 3), 4: (3, 8)}
 UNROLL = 4
 
 
@@ -20,10 +22,10 @@
     return (step + 1) // 2 * (1 - 2 * ((step + 1) % 2))
 
 
-def decode_kernel(n, dims, lens, x_hbm, wq, wk, wv, wo, kp, vp, ks_hbm, vs_hbm, out_ref, kn_out,
+def decode_kernel(n, dims, lens, x_hbm, wq, wk, wv, wo, kp, vp, ks_hbm, vs_hbm, out_ref, ks_out, vs_out,
                   x2, wqb, wkb, wvb, wob, kraw, vraw, tmp, kvsend, kvrecv, acc, qsend, qrecv, qsib, knv_send, knv_recv,
                   q32, kn32, vn32, ksuf, vsuf, suf_o, suf_m, suf_l, scr, osend, lsend, orecv, lrecv, oacc,
-                  in_sem, wsem, wosem, x_ssem, x_rsem, kv_ssem, kv_rsem, fw_ssem, q_ssem, q_rsem, sib_ssem, sib_rsem,
+                  in_sem, out_sem, wsem, wosem, x_ssem, x_rsem, kv_ssem, kv_rsem, fw_ssem, q_ssem, q_rsem, sib_ssem, sib_rsem,
                   o_ssem, o_rsem, l_ssem, l_rsem):
     rows, model, heads, group, dim, slots, pre = dims
     chips = n // CORES
@@ -90,7 +92,12 @@
         first[part].wait()
         tmp[...] = raw[...].astype(f32)
         for h in range(heads):
-            kvsend[h, part] = tmp[pl.ds(h, pre, stride=heads), :].astype(bf16)
+            block = tmp[pl.ds(h, pre, stride=heads), :]
+            if part == 0:
+                kvsend[h, 0] = block.astype(bf16)
+            else:
+                for lo in range(0, pre, dim):
+                    kvsend[h, 1, lo:lo + dim, :] = block[lo:lo + dim].T.astype(bf16)
     kvrecv[me] = kvsend[chip]
     acc[...] = jnp.zeros_like(acc)
     first[2].wait()
@@ -163,30 +170,31 @@
     for c in sib_copies():
         c.start()
 
-    def q_copy(tl, r):
-        t = core * my_heads + tl
-        return pltpu.make_async_remote_copy(qsend.at[r, tl], qrecv.at[chip], q_ssem.at[tl, r], q_rsem.at[chip],
+    def place(step):
+        return pl.ds(pl.multiple_of(step * qrows, 16), qrows)
+
+    def q_copy(step, r):
+        t = head_of(step)
+        return pltpu.make_async_remote_copy(qsend.at[r, lax.rem(t, my_heads)], qrecv.at[place(step), :], q_ssem.at[step, r], q_rsem.at[step],
                                             device_id={'ctx': t * CORES + r}, device_id_type=MESH)
 
-    def q_arrival(c):
-        return pltpu.make_async_remote_copy(qsend.at[0, 0], qrecv.at[c], q_ssem.at[0, 0], q_rsem.at[c],
+    def q_arrival(step):
+        return pltpu.make_async_remote_copy(qsend.at[0, 0], qrecv.at[place(step), :], q_ssem.at[0, 0], q_rsem.at[step],
                                             device_id={'ctx': sib}, device_id_type=MESH)
 
     q_is_local = chip // my_heads == core
 
-    @pl.loop(0, my_heads)
-    def _(i):
-        tl = lax.rem(chip + i, my_heads)
-        for r in range(CORES):
-            here = jnp.logical_and(core * my_heads + tl == chip, core == r)
-
-            @pl.when(jnp.logical_not(here))
-            def _():
-                q_copy(tl, r).start()
-
-            @pl.when(here)
-            def _():
-                qrecv[chip] = qsend[r, tl]
+    @pl.when(q_is_local)
+    def _():
+        qrecv[0:qrows, :] = qsend[core, lax.rem(chip, my_heads)]
+        q_copy(0, 1 - core).start()
+
+    @pl.loop(1, chips)
+    def _(step):
+        @pl.when(head_of(step) // my_heads == core)
+        def _():
+            for r in range(CORES):
+                q_copy(step, r).start()
 
     own = qsend[core].reshape(my_heads * qrows, dim).astype(f32)
     q32[pl.ds(pl.multiple_of(core * my_heads * qrows, 8), my_heads * qrows), :] = own
@@ -202,8 +210,6 @@
     other = pl.ds(pl.multiple_of(sib_at * my_heads * rows, 8), my_heads * rows)
     kn32[other, :] = sib_kv[0]
     vn32[other, :] = sib_kv[1]
-    kn_out[0] = kn32[...].astype(bf16)
-    kn_out[1] = vn32[...].astype(bf16)
 
     first[3].wait()
     first[4].wait()
@@ -226,6 +232,8 @@
             vb = jnp.where(hit, vn32[pl.ds(b, heads, stride=rows), :][None], vsuf[b].astype(f32).reshape(slots, heads, dim))
             kb = kb.reshape(slots * heads, dim).astype(bf16)
             vb = vb.reshape(slots * heads, dim).astype(bf16)
+            ksuf[b] = kb
+            vsuf[b] = vb
             s = lax.dot_general(qb, kb, (((1,), (1,)), ((), ())), preferred_element_type=f32)
             live = jnp.logical_and(same_head, slot_of <= length)
             s = jnp.where(live, s, -jnp.inf)
@@ -238,97 +246,59 @@
             suf_m[at, :] = jnp.broadcast_to(m * base2, (n_q, dim))
             suf_l[at, :] = jnp.broadcast_to(l, (n_q, dim))
 
+    cache_out = [pltpu.make_async_copy(ksuf, ks_out, out_sem.at[0]), pltpu.make_async_copy(vsuf, vs_out, out_sem.at[1])]
+    for c in cache_out:
+        c.start()
+
     for step in range(1, chips):
         kv_arrival(home_of(step) * CORES + core).wait_recv()
         fw_copy(step).start()
     for c in range(chips):
         kv_arrival(c * CORES + 1 - core).wait_recv()
 
-    eye = lax.broadcasted_iota(jnp.int32, (128, 128), 0) == lax.broadcasted_iota(jnp.int32, (128, 128), 1)
-
-    def o_copy(c):
-        return pltpu.make_async_remote_copy(osend.at[c], orecv.at[chip], o_ssem.at[c], o_rsem.at[chip],
-                                            device_id={'ctx': c * CORES + core}, device_id_type=MESH)
-
-    def l_copy(c):
-        return pltpu.make_async_remote_copy(lsend.at[c], lrecv.at[chip], l_ssem.at[c], l_rsem.at[chip],
-                                            device_id={'ctx': c * CORES + core}, device_id_type=MESH)
-
-    def o_arrival(t):
-        return pltpu.make_async_remote_copy(osend.at[0], orecv.at[t], o_ssem.at[0], o_rsem.at[t],
-                                            device_id={'ctx': sib}, device_id_type=MESH)
-
-    def l_arrival(t):
-        return pltpu.make_async_remote_copy(lsend.at[0], lrecv.at[t], l_ssem.at[0], l_rsem.at[t],
-                                            device_id={'ctx': sib}, device_id_type=MESH)
-
-    @pl.loop(0, chips)
-    def _(step):
-        c = home_of(step)
-
-        @pl.when(jnp.logical_not(jnp.logical_and(step == 0, q_is_local)))
-        def _():
-            q_arrival(c).wait_recv()
-
-        q = qrecv[c]
-        top = jnp.full((qrows, dim), -jnp.inf, f32)
-        for s in range(n):
-            sc = lax.dot_general(q, kvrecv[s, 0], (((1,), (1,)), ((), ())), preferred_element_type=f32)
-            scr[s] = sc
-            for b in range(0, pre, dim):
-                top = jnp.maximum(top, sc[:, b:b + dim])
-        m = top.max(axis=-1, keepdims=True) * base2
-        mass = jnp.zeros((qrows, dim), f32)
-        o = jnp.zeros((qrows, dim), f32)
-        for s in range(n):
-            p = jnp.exp2(scr[s] * base2 - m)
-            for b in range(0, pre, dim):
-                mass += p[:, b:b + dim]
-            o += jnp.dot(p.astype(bf16), kvrecv[s, 1], preferred_element_type=f32)
-        l = mass.sum(axis=-1, keepdims=True)
-        o = (o / l).astype(bf16)
-        lse = jnp.broadcast_to(m + jnp.log2(l), (qrows, dim))
-        row0 = jnp.where(eye, lse[:dim], 0.0).sum(axis=0, keepdims=True)
-        row1 = jnp.where(eye[:qrows - dim], lse[dim:], 0.0).sum(axis=0, keepdims=True)
-
-        @pl.when(step == 0)
-        def _():
-            orecv[c] = o
-            lrecv[c, 0:1, :] = row0
-            lrecv[c, 1:2, :] = row1
-
+    def o_copy(step):
+        return pltpu.make_async_remote_copy(osend.at[place(step), :], orecv.at[step], o_ssem.at[step], o_rsem.at[step],
+                                            device_id={'ctx': home_of(step) * CORES + core}, device_id_type=MESH)
+
+    def l_copy(step):
+        at = step * qrows // dim
+        return pltpu.make_async_remote_copy(lsend.at[pl.ds(at, 2)], lrecv.at[step], l_ssem.at[step], l_rsem.at[step],
+                                            device_id={'ctx': home_of(step) * CORES + core}, device_id_type=MESH)
+
+    def scores(tile, s, top):
+        q = qrecv[tile * TILE:(tile + 1) * TILE, :]
+        sc = lax.dot_general(kvrecv[s, 0], q, (((1,), (1,)), ((), ())), preferred_element_type=f32)
+        scr[tile % 2, s] = sc
+        return jnp.maximum(top, sc.reshape(pre // 8, 8, TILE).max(axis=0))
+
+    def values(tile, s, m, mass, o):
+        p = jnp.exp2(scr[tile % 2, s] * base2 - m)
+        mass += p.reshape(pre // 8, 8, TILE).sum(axis=0)
+        vt = jnp.concatenate([kvrecv[s, 1, lo:lo + dim, :] for lo in range(0, pre, dim)], axis=1)
+        return mass, o + jnp.dot(vt, p.astype(bf16), preferred_element_type=f32)
+
+    lowest = jnp.full((8, TILE), -jnp.inf, f32)
+    tiles = chips * qrows // TILE
+    row_of = lax.broadcasted_iota(jnp.int32, (qrows, 2 * dim), 0)
+    lane_of = lax.broadcasted_iota(jnp.int32, (qrows, 2 * dim), 1)
+    oacc[...] = jnp.zeros_like(oacc)
+
+    def home(step):
         @pl.when(step > 0)
         def _():
-            osend[c] = o
-            lsend[c] = jnp.zeros_like(lsend[c])
-            lsend[c, 0:1, :] = row0
-            lsend[c, 1:2, :] = row1
-            o_copy(c).start()
-            l_copy(c).start()
-
-    oacc[...] = jnp.zeros_like(oacc)
-
-    @pl.loop(0, chips)
-    def _(step):
+            o_copy(step).wait_recv()
+            l_copy(step).wait_recv()
+
         t = head_of(step)
-
-        @pl.when(step > 0)
-        def _():
-            o_arrival(t).wait_recv()
-            l_arrival(t).wait_recv()
-
-        row0 = jnp.broadcast_to(lrecv[t, 0:1, :], (dim, dim))
-        row1 = jnp.broadcast_to(lrecv[t, 1:2, :], (qrows - dim, dim))
-        lse = jnp.concatenate([
-            jnp.where(eye, row0, 0.0).sum(axis=-1, keepdims=True),
-            jnp.where(eye[:qrows - dim], row1, 0.0).sum(axis=-1, keepdims=True),
-        ], axis=0)
+        line = jnp.concatenate([lrecv[step, 0], lrecv[step, 1]], axis=1)
+        pick = lane_of == row_of + lax.rem(step * qrows, dim)
+        lse = jnp.where(pick, jnp.broadcast_to(line, (qrows, 2 * dim)), 0.0).sum(axis=-1, keepdims=True)
         at = pl.ds(pl.multiple_of(t * qrows, 8), qrows)
         sm = suf_m[at, :]
         top = jnp.maximum(lse, sm)
         wp = jnp.exp2(lse - top)
         ws = jnp.exp2(sm - top)
-        o = (wp * orecv[t].astype(f32) + ws * suf_o[at, :]) / (wp + ws * suf_l[at, :])
+        o = (wp * orecv[step].astype(f32) + ws * suf_o[at, :]) / (wp + ws * suf_l[at, :])
         o = o.astype(bf16)
         att = jnp.concatenate([o[g * rows:(g + 1) * rows] for g in range(group)], axis=1)
         out_copy(step).wait()
@@ -340,6 +310,47 @@
         def _():
             out_copy(step + OUT_SLOTS).start()
 
+    tops = None
+    arrived = 0
+    sent = 0
+    for tile in range(tiles + 1):
+        if tile < tiles:
+            while arrived * qrows < (tile + 1) * TILE:
+                if arrived == 0:
+                    @pl.when(jnp.logical_not(q_is_local))
+                    def _():
+                        q_arrival(0).wait_recv()
+                else:
+                    q_arrival(arrived).wait_recv()
+                arrived += 1
+        m = None if tile == 0 else tops.max(axis=0, keepdims=True) * base2
+        tops = lowest
+        mass = jnp.zeros((8, TILE), f32)
+        o = jnp.zeros((dim, TILE), f32)
+        for s in range(n):
+            if tile < tiles:
+                tops = scores(tile, s, tops)
+            if tile > 0:
+                mass, o = values(tile - 1, s, m, mass, o)
+        if tile > 0:
+            done = tile - 1
+            l = mass.sum(axis=0, keepdims=True)
+            o = o / l
+            lse = m + jnp.log2(l)
+            osend[done * TILE:(done + 1) * TILE, :] = o.T.astype(bf16)
+            for lo in range(0, TILE, dim):
+                lsend[(done * TILE + lo) // dim] = lse[:, lo:lo + dim]
+            while (sent + 1) * qrows <= (done + 1) * TILE:
+                if sent == 0:
+                    orecv[0] = osend[0:qrows, :]
+                    lrecv[0] = lsend[0:2]
+                else:
+                    o_copy(sent).start()
+                    l_copy(sent).start()
+                sent += 1
+            if done in HOME_AFTER:
+                pl.loop(*HOME_AFTER[done])(home)
+
     out_ref[...] = (x2[core].astype(f32) + oacc[...].astype(bf16).astype(f32)).astype(bf16)
 
     for step in range(1, chips):
@@ -347,18 +358,21 @@
     for step in range(chips):
         fw_copy(step).wait_send()
 
-    @pl.loop(0, my_heads)
-    def _(tl):
-        for r in range(CORES):
-            @pl.when(jnp.logical_not(jnp.logical_and(core * my_heads + tl == chip, core == r)))
-            def _():
-                q_copy(tl, r).wait_send()
+    @pl.when(q_is_local)
+    def _():
+        q_copy(0, 1 - core).wait_send()
 
     @pl.loop(1, chips)
     def _(step):
-        c = home_of(step)
-        o_copy(c).wait_send()
-        l_copy(c).wait_send()
+        @pl.when(head_of(step) // my_heads == core)
+        def _():
+            for r in range(CORES):
+                q_copy(step, r).wait_send()
+        o_copy(step).wait_send()
+        l_copy(step).wait_send()
+
+    for c in cache_out:
+        c.wait()
 
 
 def solution(mesh):
@@ -396,7 +410,7 @@
             vmem((n, 2, pre, dim), bf16),
             vmem((CORES * rows, (qw + 2 * heads * dim) // CORES), f32),
             vmem((CORES, my_heads, qrows, dim), bf16),
-            vmem((chips, qrows, dim), bf16),
+            vmem((chips * qrows, dim), bf16),
             vmem((my_heads, qrows, dim), bf16),
             vmem((CORES, 2, my_heads * rows, dim), bf16),
             vmem((2, my_heads * rows, dim), bf16),
@@ -408,13 +422,14 @@
             vmem((heads * qrows, dim), f32),
             vmem((heads * qrows, dim), f32),
             vmem((heads * qrows, dim), f32),
-            vmem((n, qrows, pre), f32),
+            vmem((2, n, pre, TILE), f32),
+            vmem((chips * qrows, dim), bf16),
+            vmem((chips * qrows // dim, 1, dim), f32),
             vmem((chips, qrows, dim), bf16),
-            vmem((chips, 8, dim), f32),
-            vmem((chips, qrows, dim), bf16),
-            vmem((chips, 8, dim), f32),
+            vmem((chips, 2, 1, dim), f32),
             vmem((rows, model), f32),
             dma((5,)),
+            dma((2,)),
             dma((RING, 3)),
             dma((OUT_SLOTS,)),
             dma,
@@ -422,7 +437,7 @@
             dma((chips,)),
             dma((n,)),
             dma((chips,)),
-            dma((my_heads, CORES)),
+            dma((chips, CORES)),
             dma((chips,)),
             dma((2,)),
             dma((2,)),
@@ -435,20 +450,16 @@
         vmem_spec = pl.BlockSpec(memory_space=pltpu.VMEM)
         return pl.pallas_call(
             functools.partial(decode_kernel, n, dims),
-            out_shape=(jax.ShapeDtypeStruct((rows, model), bf16), jax.ShapeDtypeStruct((2, heads * rows, dim), bf16)),
+            out_shape=(jax.ShapeDtypeStruct((rows, model), bf16),) + (jax.ShapeDtypeStruct((rows, slots * heads, dim), bf16),) * 2,
             in_specs=[pl.BlockSpec(memory_space=pltpu.SMEM)] + [any_spec] * 9,
-            out_specs=(vmem_spec, vmem_spec),
+            out_specs=(vmem_spec, any_spec, any_spec),
             scratch_shapes=scratch,
             compiler_params=pltpu.CompilerParams(collective_id=0, has_side_effects=True, vmem_limit_bytes=67_043_328),
         )(seq_lens, hidden, wq, wk, wv, wo, kp.reshape(pre * heads, dim), vp.reshape(pre * heads, dim),
           ks.reshape(rows, slots * heads, dim), vs.reshape(rows, slots * heads, dim))
 
     def local_step(hidden, seq_lens, wq, wk, wv, wo, kp, vp, ks, vs):
-        rows = hidden.shape[0]
-        _, _, slots, heads, dim = ks.shape
-        out, new = attend(hidden, seq_lens, wq, wk, wv, wo, kp, vp, ks, vs)
-        hit = (lax.broadcasted_iota(jnp.int32, (rows, slots), 1) == seq_lens[:, None])[None, :, :, None, None]
-        new = new.reshape(2, heads, rows, dim).transpose(0, 2, 1, 3)[:, None, :, None]
-        return out, jnp.where(hit, new[0], ks), jnp.where(hit, new[1], vs)
+        out, k_new, v_new = attend(hidden, seq_lens, wq, wk, wv, wo, kp, vp, ks, vs)
+        return out, k_new.reshape(ks.shape), v_new.reshape(vs.shape)
 
     return jax.shard_map(local_step, mesh=mesh, in_specs=(row_spec, lens_spec, whole_spec, whole_spec, whole_spec, whole_spec, prefix_spec, prefix_spec, cache_spec, cache_spec), out_specs=(row_spec, cache_spec, cache_spec), check_vma=False)

time: 74.2 us -> 73.1 us (0.985)
  the two profiles are of different devices: /device:TPU:21 before, /device:TPU:29 now
where the time goes in v2:
time: 73.1 us; the launch traced here: 73 us
  Pallas kernels  66 us (90%)
  local copies, waits for them, and re-layouts  6.33 us (9%)
    pallas_call x1, Pallas kernels, attend(): pl.pallas_call(functools.partial(decode_kernel, n, dims), out_shape=(jax....  66 us
    unnamed x5, local copies, waits for them, and re-layouts  6.33 us

profile of v2, /device:TPU:29, one launch (start us, length us, event | category | flops | bytes accessed | tf_op | source)
XLA Modules:
  0.0 73.0 jit_solution(3205027913209424166)
XLA Ops:
  0.6 66.0 %shard_map.121 = (bf16[32,5120]{1,0:T(8,128)(2,1)}, bf16[32,256,128]{2,1,0:T(8,128)(2,1)}, bf16[32,256,128]{2,1,0:T(8,128)(2,1)}) custom-call(s32[32]{0:T(128)} %lens.1, bf16[32,5120]{1,0:T(8,128)(2,1)} %x_hbm.1, bf16[1,5120,5120]{2,1,0:T(8,128)(2,1)} %wq.1, bf16[1,5120,1024]{2,1,0:T(8,128)(2,1)} %wk.1, bf16[1,5120,1024]{2,1,0:T(8,128)(2,1)} %wv.1, ...), custom_call_target="tpu_custom_call" | custom-call | tf_op jit(solution)/shard_map/pallas_call | solution.py:451
  66.6 1.7 %copy.16 = bf16[32,5120]{1,0:T(8,128)(2,1)} copy(bf16[32,5120]{1,0:T(8,128)(2,1)} %get-tuple-element.12) | data formatting | bytes 655360
  68.3 0.0 copy-start
  68.3 3.3 %copy.17 = bf16[1,32,32,8,128]{4,3,2,1,0:T(8,128)(2,1)} copy(bf16[1,32,32,8,128]{4,3,2,1,0:T(8,128)(2,1)} %bitcast.9) | data formatting | bytes 4194304
  71.6 0.0 copy-done
  71.6 1.3 %copy.18 = bf16[1,32,32,8,128]{4,3,2,1,0:T(8,128)(2,1)} copy(bf16[1,32,32,8,128]{4,3,2,1,0:T(8,128)(2,1)S(1)} %bitcast.8) | data formatting | bytes 4194304
Async XLA Ops:
  68.3 3.3 %copy-start = (bf16[32,256,128]{2,1,0:T(8,128)(2,1)S(1)}, bf16[32,256,128]{2,1,0:T(8,128)(2,1)}, u32[]{:S(2)}) copy-start(bf16[32,256,128]{2,1,0:T(8,128)(2,1)} %get-tuple-element.8) | copy-start | bytes 6291460

commit v3 on v2

--- a/solution.py
+++ b/solution.py
@@ -16,16 +16,19 @@
 TILE = 256
 HOME_AFTER = {2: (0, 1), 3: (1, 3), 4: (3, 8)}
 UNROLL = 4
-
-
-def hop_of(step):
-    return (step + 1) // 2 * (1 - 2 * ((step + 1) % 2))
+SENDS = 2
+PIECES = 8
+
+
+def hop_of(step, chips):
+    half = chips // 2
+    return (half - step // 2) * (1 - 2 * (step % 2)) + half * ((step + chips - 1) // chips - 1)
 
 
 def decode_kernel(n, dims, lens, x_hbm, wq, wk, wv, wo, kp, vp, ks_hbm, vs_hbm, out_ref, ks_out, vs_out,
                   x2, wqb, wkb, wvb, wob, kraw, vraw, tmp, kvsend, kvrecv, acc, qsend, qrecv, qsib, knv_send, knv_recv,
                   q32, kn32, vn32, ksuf, vsuf, suf_o, suf_m, suf_l, scr, osend, lsend, orecv, lrecv, oacc,
-                  in_sem, out_sem, wsem, wosem, x_ssem, x_rsem, kv_ssem, kv_rsem, fw_ssem, q_ssem, q_rsem, sib_ssem, sib_rsem,
+                  up_sem, in_sem, out_sem, wsem, wosem, x_ssem, x_rsem, kv_ssem, kv_rsem, fw_ssem, q_ssem, q_rsem, sib_ssem, sib_rsem,
                   o_ssem, o_rsem, l_ssem, l_rsem):
     rows, model, heads, group, dim, slots, pre = dims
     chips = n // CORES
@@ -63,10 +66,10 @@
         ]
 
     def home_of(step):
-        return lax.rem(chip + hop_of(step) + chips, chips)
+        return lax.rem(chip + hop_of(step, chips) + chips, chips)
 
     def head_of(step):
-        return lax.rem(chip - hop_of(step) + chips, chips)
+        return lax.rem(chip - hop_of(step, chips) + chips, chips)
 
     def out_copy(step):
         slot = lax.rem(step, OUT_SLOTS)
@@ -81,10 +84,12 @@
             c.start()
 
     barrier = pltpu.get_barrier_semaphore()
-
-    @pl.loop(1, n)
-    def _(d):
-        pl.semaphore_signal(barrier, inc=1, device_id={'ctx': lax.rem(me + d, n)}, device_id_type=MESH)
+    pl.semaphore_signal(barrier, inc=1, device_id={'ctx': sib}, device_id_type=MESH)
+    for t in range(1, chips):
+        @pl.when(t > chip)
+        def _():
+            for r in range(CORES):
+                pl.semaphore_signal(barrier, inc=1, device_id={'ctx': t * CORES + r}, device_id_type=MESH)
 
     for c in first[3:]:
         c.start()
@@ -99,16 +104,19 @@
                 for lo in range(0, pre, dim):
                     kvsend[h, 1, lo:lo + dim, :] = block[lo:lo + dim].T.astype(bf16)
     kvrecv[me] = kvsend[chip]
-    acc[...] = jnp.zeros_like(acc)
     first[2].wait()
-    pl.semaphore_wait(barrier, n - 1)
+    pl.semaphore_wait(barrier, chip * CORES + 1)
+    for t in range(chips - 1):
+        @pl.when(t < chip)
+        def _():
+            for r in range(CORES):
+                pl.semaphore_signal(up_sem.at[chip], inc=1, device_id={'ctx': t * CORES + r}, device_id_type=MESH)
 
     x_copy = pltpu.make_async_remote_copy(x2.at[core], x2.at[core], x_ssem, x_rsem, device_id={'ctx': sib}, device_id_type=MESH)
     x_copy.start()
 
-    def kv_copy(step):
-        t = home_of(step)
-        return pltpu.make_async_remote_copy(kvsend.at[t], kvrecv.at[me], kv_ssem.at[step], kv_rsem.at[me],
+    def kv_copy(t):
+        return pltpu.make_async_remote_copy(kvsend.at[t], kvrecv.at[me], kv_ssem.at[t], kv_rsem.at[me],
                                             device_id={'ctx': t * CORES + core}, device_id_type=MESH)
 
     def fw_copy(step):
@@ -122,8 +130,13 @@
                                             device_id={'ctx': sib}, device_id_type=MESH)
 
     for step in range(1, chips):
-        kv_copy(step).start()
+        t = home_of(step)
+
+        @pl.when(t < chip)
+        def _():
+            kv_copy(t).start()
     fw_copy(0).start()
+    acc[...] = jnp.zeros_like(acc)
     x_copy.wait()
 
     @pl.loop(0, steps)
@@ -136,6 +149,14 @@
             acc[:, b:b + 512] += jnp.dot(xc, wqb[slot, :, b:b + 512], preferred_element_type=f32)
         acc[:, q_half:q_half + kv_half] += jnp.dot(xc, wkb[slot], preferred_element_type=f32)
         acc[:, q_half + kv_half:] += jnp.dot(xc, wvb[slot], preferred_element_type=f32)
+
+        for i in range(SENDS):
+            t = chip + 1 + j * SENDS + i
+
+            @pl.when(t < chips)
+            def _():
+                pl.semaphore_wait(up_sem.at[t], CORES)
+                kv_copy(t).start()
 
         @pl.when(j + RING < steps)
         def _():
@@ -354,7 +375,7 @@
     out_ref[...] = (x2[core].astype(f32) + oacc[...].astype(bf16).astype(f32)).astype(bf16)
 
     for step in range(1, chips):
-        kv_copy(step).wait_send()
+        kv_copy(home_of(step)).wait_send()
     for step in range(chips):
         fw_copy(step).wait_send()
 
@@ -373,6 +394,42 @@
 
     for c in cache_out:
         c.wait()
+
+
+def publish_kernel(ins, outs, bufs, in_sem, out_sem):
+    pieces = []
+    for a in range(3):
+        count = PIECES if a else 1
+        size = ins[a].shape[0] // count
+        for i in range(count):
+            at = pl.ds(i * size, size)
+            k = len(pieces)
+            pieces.append((pltpu.make_async_copy(ins[a].at[at], bufs[a].at[at], in_sem.at[k]),
+                           pltpu.make_async_copy(bufs[a].at[at], outs[a].at[at], out_sem.at[k])))
+    for c, _ in pieces:
+        c.start()
+    for c, d in pieces:
+        c.wait()
+        d.start()
+    for _, d in pieces:
+        d.wait()
+
+
+def publish(arrays):
+    any_spec = pl.BlockSpec(memory_space=pl.ANY)
+    count = 1 + 2 * PIECES
+
+    def kernel(a, b, c, x, y, z, p, q, r, in_sem, out_sem):
+        publish_kernel((a, b, c), (x, y, z), (p, q, r), in_sem, out_sem)
+
+    return pl.pallas_call(
+        kernel,
+        out_shape=tuple(jax.ShapeDtypeStruct(a.shape, a.dtype) for a in arrays),
+        in_specs=[any_spec] * 3,
+        out_specs=(any_spec,) * 3,
+        scratch_shapes=[pltpu.VMEM(a.shape, a.dtype) for a in arrays] + [pltpu.SemaphoreType.DMA((count,))] * 2,
+        compiler_params=pltpu.CompilerParams(vmem_limit_bytes=67_043_328),
+    )(*arrays)
 
 
 def solution(mesh):
@@ -428,6 +485,7 @@
             vmem((chips, qrows, dim), bf16),
             vmem((chips, 2, 1, dim), f32),
             vmem((rows, model), f32),
+            pltpu.SemaphoreType.REGULAR((chips,)),
             dma((5,)),
             dma((2,)),
             dma((RING, 3)),
@@ -459,7 +517,7 @@
           ks.reshape(rows, slots * heads, dim), vs.reshape(rows, slots * heads, dim))
 
     def local_step(hidden, seq_lens, wq, wk, wv, wo, kp, vp, ks, vs):
-        out, k_new, v_new = attend(hidden, seq_lens, wq, wk, wv, wo, kp, vp, ks, vs)
+        out, k_new, v_new = publish(attend(hidden, seq_lens, wq, wk, wv, wo, kp, vp, ks, vs))
         return out, k_new.reshape(ks.shape), v_new.reshape(vs.shape)
 
     return jax.shard_map(local_step, mesh=mesh, in_specs=(row_spec, lens_spec, whole_spec, whole_spec, whole_spec, whole_spec, prefix_spec, prefix_spec, cache_spec, cache_spec), out_specs=(row_spec, cache_spec, cache_spec), check_vma=False)

time: 73.1 us -> 70.7 us (0.967)
  the two profiles are of different devices: /device:TPU:29 before, /device:TPU:21 now
where the time goes in v3:
time: 70.7 us; the launch traced here: 70.2 us
  Pallas kernels  69.6 us (98%)
    pallas_call x1, Pallas kernels, attend(): pl.pallas_call(functools.partial(decode_kernel, n, dims), out_shape=(jax....  65.4 us
    pallas_call x1, Pallas kernels, publish(): pl.pallas_call(kernel, out_shape=tuple((jax.ShapeDtypeStruct(a.shape, a.d...  4.16 us

profile of v3, /device:TPU:21, one launch (start us, length us, event | category | flops | bytes accessed | tf_op | source)
XLA Modules:
  0.0 70.2 jit_solution(1073984014051594483)
XLA Ops:
  0.6 65.4 %shard_map.121 = (bf16[32,5120]{1,0:T(8,128)(2,1)}, bf16[32,256,128]{2,1,0:T(8,128)(2,1)}, bf16[32,256,128]{2,1,0:T(8,128)(2,1)}) custom-call(s32[32]{0:T(128)} %lens.1, bf16[32,5120]{1,0:T(8,128)(2,1)} %x_hbm.1, bf16[1,5120,5120]{2,1,0:T(8,128)(2,1)} %wq.1, bf16[1,5120,1024]{2,1,0:T(8,128)(2,1)} %wk.1, bf16[1,5120,1024]{2,1,0:T(8,128)(2,1)} %wv.1, ...), custom_call_target="tpu_custom_call" | custom-call | tf_op jit(solution)/shard_map/pallas_call | solution.py:509
  66.1 4.2 %shard_map.122 = (bf16[32,5120]{1,0:T(8,128)(2,1)}, bf16[32,256,128]{2,1,0:T(8,128)(2,1)}, bf16[32,256,128]{2,1,0:T(8,128)(2,1)}) custom-call(bf16[32,5120]{1,0:T(8,128)(2,1)} %get-tuple-element.9.a, bf16[32,256,128]{2,1,0:T(8,128)(2,1)} %get-tuple-element.10.b, bf16[32,256,128]{2,1,0:T(8,128)(2,1)} %get-tuple-element.11.c), custom_call_target="tpu_custom_call" | custom-call | tf_op jit(solution)/shard_map/pallas_call | solution.py:425

commit v4 on v3

--- a/solution.py
+++ b/solution.py
@@ -10,13 +10,12 @@
 
 MESH = pl.DeviceIdType.MESH
 CORES = 2
-CHUNK = 512
-RING = 3
-OUT_SLOTS = 4
+CHUNK = 256
+RING = 4
+OUT_SLOTS = 5
 TILE = 256
-HOME_AFTER = {2: (0, 1), 3: (1, 3), 4: (3, 8)}
+
 UNROLL = 4
-SENDS = 2
 PIECES = 8
 
 
@@ -71,17 +70,17 @@
     def head_of(step):
         return lax.rem(chip - hop_of(step, chips) + chips, chips)
 
+    def near_of(step):
+        return lax.rem(chip + (step + 1) // 2 * (1 - 2 * ((step + 1) % 2)) + chips, chips)
+
     def out_copy(step):
         slot = lax.rem(step, OUT_SLOTS)
         r = pl.ds(pl.multiple_of(head_of(step) * out_rows, out_rows), out_rows)
         return pltpu.make_async_copy(wo.at[0, r, :], wob.at[slot], wosem.at[slot])
 
     first = loads()
-    for c in first[:3]:
+    for c in first[:2]:
         c.start()
-    for s in range(RING):
-        for c in weight_copies(s, s):
-            c.start()
 
     barrier = pltpu.get_barrier_semaphore()
     pl.semaphore_signal(barrier, inc=1, device_id={'ctx': sib}, device_id_type=MESH)
@@ -91,10 +90,22 @@
             for r in range(CORES):
                 pl.semaphore_signal(barrier, inc=1, device_id={'ctx': t * CORES + r}, device_id_type=MESH)
 
-    for c in first[3:]:
-        c.start()
+    pl.semaphore_wait(barrier, chip * CORES + 1)
+    for t in range(chips - 1):
+        @pl.when(t < chip)
+        def _():
+            for r in range(CORES):
+                pl.semaphore_signal(up_sem.at[chip], inc=1, device_id={'ctx': t * CORES + r}, device_id_type=MESH)
+
     for part, raw in ((0, kraw), (1, vraw)):
         first[part].wait()
+        if part == 1:
+            first[2].start()
+            for s in range(RING):
+                for c in weight_copies(s, s):
+                    c.start()
+            for c in first[3:]:
+                c.start()
         tmp[...] = raw[...].astype(f32)
         for h in range(heads):
             block = tmp[pl.ds(h, pre, stride=heads), :]
@@ -104,23 +115,14 @@
                 for lo in range(0, pre, dim):
                     kvsend[h, 1, lo:lo + dim, :] = block[lo:lo + dim].T.astype(bf16)
     kvrecv[me] = kvsend[chip]
-    first[2].wait()
-    pl.semaphore_wait(barrier, chip * CORES + 1)
-    for t in range(chips - 1):
-        @pl.when(t < chip)
-        def _():
-            for r in range(CORES):
-                pl.semaphore_signal(up_sem.at[chip], inc=1, device_id={'ctx': t * CORES + r}, device_id_type=MESH)
-
     x_copy = pltpu.make_async_remote_copy(x2.at[core], x2.at[core], x_ssem, x_rsem, device_id={'ctx': sib}, device_id_type=MESH)
-    x_copy.start()
 
     def kv_copy(t):
         return pltpu.make_async_remote_copy(kvsend.at[t], kvrecv.at[me], kv_ssem.at[t], kv_rsem.at[me],
                                             device_id={'ctx': t * CORES + core}, device_id_type=MESH)
 
     def fw_copy(step):
-        j = home_of(step) * CORES + core
+        j = near_of(step) * CORES + core
         src = kvsend.at[chip] if step == 0 else kvrecv.at[j]
         return pltpu.make_async_remote_copy(src, kvrecv.at[j], fw_ssem.at[step], kv_rsem.at[j],
                                             device_id={'ctx': sib}, device_id_type=MESH)
@@ -130,12 +132,16 @@
                                             device_id={'ctx': sib}, device_id_type=MESH)
 
     for step in range(1, chips):
-        t = home_of(step)
-
-        @pl.when(t < chip)
-        def _():
-            kv_copy(t).start()
+        t = near_of(step)
+
+        @pl.when(t > chip)
+        def _():
+            pl.semaphore_wait(up_sem.at[t], CORES)
+
+        kv_copy(t).start()
     fw_copy(0).start()
+    first[2].wait()
+    x_copy.start()
     acc[...] = jnp.zeros_like(acc)
     x_copy.wait()
 
@@ -149,14 +155,6 @@
             acc[:, b:b + 512] += jnp.dot(xc, wqb[slot, :, b:b + 512], preferred_element_type=f32)
         acc[:, q_half:q_half + kv_half] += jnp.dot(xc, wkb[slot], preferred_element_type=f32)
         acc[:, q_half + kv_half:] += jnp.dot(xc, wvb[slot], preferred_element_type=f32)
-
-        for i in range(SENDS):
-            t = chip + 1 + j * SENDS + i
-
-            @pl.when(t < chips)
-            def _():
-                pl.semaphore_wait(up_sem.at[t], CORES)
-                kv_copy(t).start()
 
         @pl.when(j + RING < steps)
         def _():
@@ -194,28 +192,22 @@
     def place(step):
         return pl.ds(pl.multiple_of(step * qrows, 16), qrows)
 
-    def q_copy(step, r):
+    def q_copy(step, src):
         t = head_of(step)
-        return pltpu.make_async_remote_copy(qsend.at[r, lax.rem(t, my_heads)], qrecv.at[place(step), :], q_ssem.at[step, r], q_rsem.at[step],
-                                            device_id={'ctx': t * CORES + r}, device_id_type=MESH)
-
-    def q_arrival(step):
-        return pltpu.make_async_remote_copy(qsend.at[0, 0], qrecv.at[place(step), :], q_ssem.at[0, 0], q_rsem.at[step],
-                                            device_id={'ctx': sib}, device_id_type=MESH)
-
-    q_is_local = chip // my_heads == core
-
-    @pl.when(q_is_local)
-    def _():
-        qrecv[0:qrows, :] = qsend[core, lax.rem(chip, my_heads)]
-        q_copy(0, 1 - core).start()
-
-    @pl.loop(1, chips)
-    def _(step):
-        @pl.when(head_of(step) // my_heads == core)
-        def _():
-            for r in range(CORES):
-                q_copy(step, r).start()
+        return pltpu.make_async_remote_copy(src.at[lax.rem(t, my_heads)], qrecv.at[place(step), :], q_ssem.at[step], q_rsem.at[step],
+                                            device_id={'ctx': t * CORES + core}, device_id_type=MESH)
+
+    def send_queries(half, src):
+        @pl.when(chip // my_heads == half)
+        def _():
+            qrecv[0:qrows, :] = src[lax.rem(chip, my_heads)]
+
+        @pl.loop(1, chips)
+        def _(step):
+            @pl.when(head_of(step) // my_heads == half)
+            def _():
+                q_copy(step, src).start()
+
 
     own = qsend[core].reshape(my_heads * qrows, dim).astype(f32)
     q32[pl.ds(pl.multiple_of(core * my_heads * qrows, 8), my_heads * qrows), :] = own
@@ -272,7 +264,12 @@
         c.start()
 
     for step in range(1, chips):
-        kv_arrival(home_of(step) * CORES + core).wait_recv()
+        kv_copy(near_of(step)).wait_send()
+    send_queries(core, qsend.at[core])
+    send_queries(1 - core, qsib)
+
+    for step in range(1, chips):
+        kv_arrival(near_of(step) * CORES + core).wait_recv()
         fw_copy(step).start()
     for c in range(chips):
         kv_arrival(c * CORES + 1 - core).wait_recv()
@@ -305,8 +302,7 @@
     oacc[...] = jnp.zeros_like(oacc)
 
     def home(step):
-        @pl.when(step > 0)
-        def _():
+        if not isinstance(step, int):
             o_copy(step).wait_recv()
             l_copy(step).wait_recv()
 
@@ -337,12 +333,8 @@
     for tile in range(tiles + 1):
         if tile < tiles:
             while arrived * qrows < (tile + 1) * TILE:
-                if arrived == 0:
-                    @pl.when(jnp.logical_not(q_is_local))
-                    def _():
-                        q_arrival(0).wait_recv()
-                else:
-                    q_arrival(arrived).wait_recv()
+                if arrived > 0:
+                    q_copy(arrived, qsib).wait_recv()
                 arrived += 1
         m = None if tile == 0 else tops.max(axis=0, keepdims=True) * base2
         tops = lowest
@@ -369,26 +361,18 @@
                     o_copy(sent).start()
                     l_copy(sent).start()
                 sent += 1
-            if done in HOME_AFTER:
-                pl.loop(*HOME_AFTER[done])(home)
-
+            if done == 2:
+                home(0)
+
+    pl.loop(1, chips)(home)
     out_ref[...] = (x2[core].astype(f32) + oacc[...].astype(bf16).astype(f32)).astype(bf16)
 
-    for step in range(1, chips):
-        kv_copy(home_of(step)).wait_send()
     for step in range(chips):
         fw_copy(step).wait_send()
 
-    @pl.when(q_is_local)
-    def _():
-        q_copy(0, 1 - core).wait_send()
-
     @pl.loop(1, chips)
     def _(step):
-        @pl.when(head_of(step) // my_heads == core)
-        def _():
-            for r in range(CORES):
-                q_copy(step, r).wait_send()
+        q_copy(step, qsib).wait_send()
         o_copy(step).wait_send()
         l_copy(step).wait_send()
 
@@ -495,7 +479,7 @@
             dma((chips,)),
             dma((n,)),
             dma((chips,)),
-            dma((chips, CORES)),
+            dma((chips,)),
             dma((chips,)),
             dma((2,)),
             dma((2,)),

time: 70.7 us -> 68.4 us (0.967)
  Pallas kernels: 69.6 us -> 66.9 us
    pallas_call x1, Pallas kernels: 65.4 us -> 62.7 us  [attend(): pl.pallas_call(functools.partial(decode_kernel, n, dims), out_shape=(jax....]
where the time goes in v4:
time: 68.4 us; the launch traced here: 67.5 us
  Pallas kernels  66.9 us (98%)
    pallas_call x1, Pallas kernels, attend(): pl.pallas_call(functools.partial(decode_kernel, n, dims), out_shape=(jax....  62.7 us
    pallas_call x1, Pallas kernels, publish(): pl.pallas_call(kernel, out_shape=tuple((jax.ShapeDtypeStruct(a.shape, a.d...  4.16 us

profile of v4, /device:TPU:21, one launch (start us, length us, event | category | flops | bytes accessed | tf_op | source)
XLA Modules:
  0.0 67.5 jit_solution(12029569011979413500)
XLA Ops:
  0.6 62.7 %shard_map.121 = (bf16[32,5120]{1,0:T(8,128)(2,1)}, bf16[32,256,128]{2,1,0:T(8,128)(2,1)}, bf16[32,256,128]{2,1,0:T(8,128)(2,1)}) custom-call(s32[32]{0:T(128)} %lens.1, bf16[32,5120]{1,0:T(8,128)(2,1)} %x_hbm.1, bf16[1,5120,5120]{2,1,0:T(8,128)(2,1)} %wq.1, bf16[1,5120,1024]{2,1,0:T(8,128)(2,1)} %wk.1, bf16[1,5120,1024]{2,1,0:T(8,128)(2,1)} %wv.1, ...), custom_call_target="tpu_custom_call" | custom-call | tf_op jit(solution)/shard_map/pallas_call | solution.py:493
  63.4 4.2 %shard_map.122 = (bf16[32,5120]{1,0:T(8,128)(2,1)}, bf16[32,256,128]{2,1,0:T(8,128)(2,1)}, bf16[32,256,128]{2,1,0:T(8,128)(2,1)}) custom-call(bf16[32,5120]{1,0:T(8,128)(2,1)} %get-tuple-element.9.a, bf16[32,256,128]{2,1,0:T(8,128)(2,1)} %get-tuple-element.10.b, bf16[32,256,128]{2,1,0:T(8,128)(2,1)} %get-tuple-element.11.c), custom_call_target="tpu_custom_call" | custom-call | tf_op jit(solution)/shard_map/pallas_call | solution.py:409

commit v5 on v4

--- a/solution.py
+++ b/solution.py
@@ -19,9 +19,8 @@
 PIECES = 8
 
 
-def hop_of(step, chips):
-    half = chips // 2
-    return (half - step // 2) * (1 - 2 * (step % 2)) + half * ((step + chips - 1) // chips - 1)
+def hop_of(step):
+    return (step + 1) // 2 * (1 - 2 * ((step + 1) % 2))
 
 
 def decode_kernel(n, dims, lens, x_hbm, wq, wk, wv, wo, kp, vp, ks_hbm, vs_hbm, out_ref, ks_out, vs_out,
@@ -65,10 +64,10 @@
         ]
 
     def home_of(step):
-        return lax.rem(chip + hop_of(step, chips) + chips, chips)
+        return lax.rem(chip + hop_of(step) + chips, chips)
 
     def head_of(step):
-        return lax.rem(chip - hop_of(step, chips) + chips, chips)
+        return lax.rem(chip - hop_of(step) + chips, chips)
 
     def near_of(step):
         return lax.rem(chip + (step + 1) // 2 * (1 - 2 * ((step + 1) % 2)) + chips, chips)
@@ -234,8 +233,7 @@
     slot_of = col_id >> int(math.log2(heads))
     slot3 = lax.broadcasted_iota(jnp.int32, (slots, heads, dim), 0)
 
-    @pl.loop(0, rows // UNROLL)
-    def _(i):
+    def suffix(i):
         for u in range(UNROLL):
             b = i * UNROLL + u
             length = lens[b]
@@ -259,14 +257,15 @@
             suf_m[at, :] = jnp.broadcast_to(m * base2, (n_q, dim))
             suf_l[at, :] = jnp.broadcast_to(l, (n_q, dim))
 
+    early = rows // UNROLL * 3 // 4
+    pl.loop(0, early)(suffix)
+    send_queries(core, qsend.at[core])
+    send_queries(1 - core, qsib)
+    pl.loop(early, rows // UNROLL)(suffix)
+
     cache_out = [pltpu.make_async_copy(ksuf, ks_out, out_sem.at[0]), pltpu.make_async_copy(vsuf, vs_out, out_sem.at[1])]
     for c in cache_out:
         c.start()
-
-    for step in range(1, chips):
-        kv_copy(near_of(step)).wait_send()
-    send_queries(core, qsend.at[core])
-    send_queries(1 - core, qsib)
 
     for step in range(1, chips):
         kv_arrival(near_of(step) * CORES + core).wait_recv()
@@ -361,12 +360,13 @@
                     o_copy(sent).start()
                     l_copy(sent).start()
                 sent += 1
-            if done == 2:
-                home(0)
-
+
+    home(0)
     pl.loop(1, chips)(home)
     out_ref[...] = (x2[core].astype(f32) + oacc[...].astype(bf16).astype(f32)).astype(bf16)
 
+    for step in range(1, chips):
+        kv_copy(near_of(step)).wait_send()
     for step in range(chips):
         fw_copy(step).wait_send()
 

time: 68.4 us -> 65 us (0.950)
  Pallas kernels: 66.9 us -> 63.8 us
    pallas_call x1, Pallas kernels: 62.7 us -> 59.6 us  [attend(): pl.pallas_call(functools.partial(decode_kernel, n, dims), out_shape=(jax....]
where the time goes in v5:
time: 65 us; the launch traced here: 64.4 us
  Pallas kernels  63.8 us (98%)
    pallas_call x1, Pallas kernels, attend(): pl.pallas_call(functools.partial(decode_kernel, n, dims), out_shape=(jax....  59.6 us
    pallas_call x1, Pallas kernels, publish(): pl.pallas_call(kernel, out_shape=tuple((jax.ShapeDtypeStruct(a.shape, a.d...  4.16 us

profile of v5, /device:TPU:21, one launch (start us, length us, event | category | flops | bytes accessed | tf_op | source)
XLA Modules:
  0.0 64.4 jit_solution(9711910523570776979)
XLA Ops:
  0.6 59.6 %shard_map.121 = (bf16[32,5120]{1,0:T(8,128)(2,1)}, bf16[32,256,128]{2,1,0:T(8,128)(2,1)}, bf16[32,256,128]{2,1,0:T(8,128)(2,1)}) custom-call(s32[32]{0:T(128)} %lens.1, bf16[32,5120]{1,0:T(8,128)(2,1)} %x_hbm.1, bf16[1,5120,5120]{2,1,0:T(8,128)(2,1)} %wq.1, bf16[1,5120,1024]{2,1,0:T(8,128)(2,1)} %wk.1, bf16[1,5120,1024]{2,1,0:T(8,128)(2,1)} %wv.1, ...), custom_call_target="tpu_custom_call" | custom-call | tf_op jit(solution)/shard_map/pallas_call | solution.py:493
  60.3 4.2 %shard_map.122 = (bf16[32,5120]{1,0:T(8,128)(2,1)}, bf16[32,256,128]{2,1,0:T(8,128)(2,1)}, bf16[32,256,128]{2,1,0:T(8,128)(2,1)}) custom-call(bf16[32,5120]{1,0:T(8,128)(2,1)} %get-tuple-element.9.a, bf16[32,256,128]{2,1,0:T(8,128)(2,1)} %get-tuple-element.10.b, bf16[32,256,128]{2,1,0:T(8,128)(2,1)} %get-tuple-element.11.c), custom_call_target="tpu_custom_call" | custom-call | tf_op jit(solution)/shard_map/pallas_call | solution.py:409
